TPU v7x, 32 devices: a whole 2x2x4 slice. The times are simulated.
32 devices in a mesh: grp: 2 (over core), dev: 16 (over z, y, x).
Axes of the slice: x: 2, y: 2, z: 4, core: 2. Of those that a mesh axis runs over, the one named last changes fastest.
Arguments:
- accum: float32 [4096, 24, 128], P(('grp', 'dev')), may hold values from -48 to 48
- step_count: int32 [24], replicated, may hold values from 1 to 12
- stretch_slot: int32 [4096], replicated, may hold values from 0 to 4095, as said below
- span_length: int32 [32], replicated, may hold values from 1 to 256, 4096 in all
- wet_mask: int32 [8192], P(('grp', 'dev')), may hold values 0 or 1
Outputs:
- ocean_flux: float32 [8192, 24, 128], P(('grp', 'dev'))
Inputs may be any that keep to these rules, and one draw needn't show every extreme that they name: `stretch_slot`: A permutation of the slots; any 32 consecutive row blocks lie on 32 different atmosphere devices (slot // 128). `span_length`: sums to 4096; some ocean device owns exactly 256 blocks. `wet_mask`: entries of slots beyond an ocean device's span are ignored.
All inputs are finite; a program needn't handle non-finite values.
Results may differ from a plain program's by a relative error of at most 0.000071.
Values sent between devices are 32-bit elements; how exact they have to be, the bound alone decides.
A program may use at most 64 MiB of HBM per device.

v0:
```python
import functools
import jax
import jax.numpy as jnp
from jax import lax
from jax.experimental import pallas as pl
from jax.experimental.pallas import tpu as pltpu
from jax.sharding import PartitionSpec as P

MESH = pl.DeviceIdType.MESH
ROOMS = (36, 38, 40, 42, 44, 48)


def exchange_kernel(
    sizes, stretch, spans, wet, accum, received, halo,
    starts, packed, landed, edge_out, edge_in, send_sem, recv_sem, out_sem, edge_send, edge_recv, edge_copy,
):
    groups, chips, layers, pair_most, blocks_dev, all_blocks = sizes
    devices = groups * chips
    plane = chips // layers
    grp = lax.axis_index("grp")
    dev = lax.axis_index("dev")
    me = grp * chips + dev
    layer, place = dev // plane, dev % plane

    def at(index):
        return (index // chips, index % chips)

    barrier = pltpu.get_barrier_semaphore()

    @pl.loop(1, devices)
    def _(step):
        pl.semaphore_signal(barrier, inc=1, device_id=at((me + step) % devices), device_id_type=MESH)

    def prefix(owner, total):
        starts[owner] = total
        return total + spans[owner]

    lax.fori_loop(0, devices, prefix, jnp.int32(0))

    def find(block, found):
        return jnp.where(stretch[block] // blocks_dev == me, block, found)

    phase = lax.fori_loop(0, devices, find, jnp.int32(0), unroll=8)

    def partner(turn, rest):
        there = ((layer + turn) % layers) * plane + (place + rest % plane) % plane
        return ((grp + rest // plane) % groups) * chips + there

    def pack(owner, target, base):
        start = starts[owner]
        first = start + lax.rem(phase - start + all_blocks * devices, devices)
        for rank in range(pair_most):
            block = jnp.minimum(first + rank * devices, all_blocks - 1)
            slot = lax.rem(stretch[block], blocks_dev)
            target[base + rank] = accum[slot]

    def send_copy(other):
        return pltpu.make_async_remote_copy(
            src_ref=packed.at[pl.ds(other * pair_most, pair_most)],
            dst_ref=landed.at[pl.ds(me * pair_most, pair_most)],
            send_sem=send_sem.at[other],
            recv_sem=recv_sem.at[me],
            device_id=at(other),
            device_id_type=MESH,
        )

    def out_copy(other):
        return pltpu.make_async_copy(
            landed.at[pl.ds(other * pair_most, pair_most)],
            received.at[pl.ds(other * pair_most, pair_most)],
            out_sem.at[other],
        )

    turns = [layers // 2] + [t for t in range(1, layers) if t != layers // 2]
    if layers > 1:
        turns = turns + [0]
    else:
        turns = [0]
    rests = groups * plane
    for number, turn in enumerate(turns):
        low = 1 if turn == 0 else 0

        @pl.loop(low, rests)
        def _(rest):
            other = partner(turn, rest)
            pack(other, packed, other * pair_most)

        if number == 0:
            pl.semaphore_wait(barrier, devices - 1)

        @pl.loop(low, rests)
        def _(rest):
            send_copy(partner(turn, rest)).start()

    pack(me, landed, me * pair_most)

    for turn in reversed(turns):
        low = 1 if turn == 0 else 0

        @pl.loop(low, rests)
        def _(rest):
            other = partner(turn, rest)
            pltpu.make_async_remote_copy(
                src_ref=packed.at[pl.ds(other * pair_most, pair_most)],
                dst_ref=landed.at[pl.ds(other * pair_most, pair_most)],
                send_sem=send_sem.at[other],
                recv_sem=recv_sem.at[other],
                device_id=at(other),
                device_id_type=MESH,
            ).wait_recv()
            out_copy(other).start()

    out_copy(me).start()

    start = starts[me]
    length = spans[me]
    first_from = stretch[start] // blocks_dev
    last = jnp.maximum(length - 1, 0)
    last_from = stretch[start + last] // blocks_dev
    edge_out[0] = landed[last_from * pair_most + last // devices] * (
        wet[last] == 1
    ).astype(jnp.float32)
    edge_out[1] = landed[first_from * pair_most] * (wet[0] == 1).astype(jnp.float32)
    copies = []
    for side, shift in ((0, 1), (1, devices - 1)):
        copies.append(
            pltpu.make_async_remote_copy(
                src_ref=edge_out.at[side],
                dst_ref=edge_in.at[side],
                send_sem=edge_send.at[side],
                recv_sem=edge_recv.at[side],
                device_id=at((me + shift) % devices),
                device_id_type=MESH,
            )
        )
    for copy in copies:
        copy.start()

    @pl.loop(1, devices)
    def _(step):
        send_copy((me + step) % devices).wait_send()

    @pl.loop(0, devices)
    def _(other):
        out_copy(other).wait()

    for copy in copies:
        copy.wait()
    final = pltpu.make_async_copy(edge_in, halo, edge_copy)
    final.start()
    final.wait()


def relay_kernel(
    sizes, room, stretch, spans, wet, accum, received, halo,
    starts, packed, relay_one, relay_two, relay_three, forward, landed, edge_out, edge_in,
    far_send, far_recv, send_sem, recv_sem, out_sem, edge_send, edge_recv, edge_copy,
):
    groups, chips, layers, pair_most, blocks_dev, all_blocks = sizes
    devices = groups * chips
    plane = chips // layers
    rests = groups * plane
    relayed = (None, relay_one, relay_two, relay_three)
    grp = lax.axis_index("grp")
    dev = lax.axis_index("dev")
    me = grp * chips + dev
    layer, place = dev // plane, dev % plane
    across = (layer, layer + 1 - 2 * (layer % 2), (layer + 2) % 4, 3 - layer)

    def at(index):
        return (index // chips, index % chips)

    barrier = pltpu.get_barrier_semaphore()

    @pl.loop(1, devices)
    def _(step):
        pl.semaphore_signal(barrier, inc=1, device_id=at((me + step) % devices), device_id_type=MESH)

    def prefix(owner, total):
        starts[owner] = total
        return total + spans[owner]

    starts[devices] = lax.fori_loop(0, devices, prefix, jnp.int32(0))

    def find(block, found):
        holder = stretch[block] // blocks_dev
        base = grp * chips + place
        return tuple(
            jnp.where(holder == base + across[turn] * plane, block, found[turn]) for turn in range(4)
        )

    phases = lax.fori_loop(0, devices, find, (jnp.int32(0),) * 4, unroll=8)

    def first_of(phase, start):
        return start + lax.rem(phase - start + all_blocks * devices, devices)

    def ranges(phase, target):
        firsts, amount = [], None
        for part in range(2):
            low = part * chips + target * plane
            first = first_of(phase, starts[low])
            firsts.append(first)
            if part == 0:
                amount = (starts[low + plane] - first + devices - 1) // devices
        return firsts, amount

    def slot_of(block):
        return lax.rem(stretch[jnp.minimum(block, all_blocks - 1)], blocks_dev)

    def far_copy(turn):
        return pltpu.make_async_remote_copy(
            src_ref=packed.at[turn - 1],
            dst_ref=relayed[turn],
            send_sem=far_send.at[turn - 1],
            recv_sem=far_recv.at[turn - 1],
            device_id=at(grp * chips + across[turn] * plane + place),
            device_id_type=MESH,
        )

    for turn in (1, 2, 3):
        (first_low, first_high), amount = ranges(phases[0], across[turn])

        def fill(spot, carry, turn=turn, first_low=first_low, first_high=first_high, amount=amount):
            block = jnp.where(
                spot < amount, first_low + devices * spot, first_high + devices * (spot - amount)
            )
            packed[turn - 1, spot] = accum[slot_of(block)]
            return carry

        lax.fori_loop(0, room, fill, jnp.int32(0), unroll=2)
        if turn == 1:
            pl.semaphore_wait(barrier, devices - 1)
        far_copy(turn).start()

    def mate(rest):
        return ((grp + rest // plane) % groups) * chips + layer * plane + (place + rest % plane) % plane

    def shifted(index, turn):
        return index + (across[turn] - layer) * plane

    def near_copy(turn, rest, sender):
        return pltpu.make_async_remote_copy(
            src_ref=forward.at[pl.ds((turn * rests + rest) * pair_most, pair_most)],
            dst_ref=landed.at[pl.ds(sender * pair_most, pair_most)],
            send_sem=send_sem.at[turn * rests + rest],
            recv_sem=recv_sem.at[sender],
            device_id=at(mate(rest)),
            device_id_type=MESH,
        )

    def out_copy(other):
        return pltpu.make_async_copy(
            landed.at[pl.ds(other * pair_most, pair_most)],
            received.at[pl.ds(other * pair_most, pair_most)],
            out_sem.at[other],
        )

    def hand_on(turn):
        phase = phases[turn]
        sender = shifted(me, turn)
        if turn > 0:
            (first_low, first_high), amount = ranges(phase, layer)

        def put(owner, target, base):
            first = first_of(phase, starts[owner])
            if turn == 0:
                for rank in range(pair_most):
                    target[base + rank] = accum[slot_of(first + rank * devices)]
            else:
                in_low = owner < chips
                spot = jnp.where(in_low, first - first_low, first - first_high) // devices
                spot = spot + jnp.where(in_low, 0, amount)
                for rank in range(pair_most):
                    target[base + rank] = relayed[turn][jnp.clip(spot + rank, 0, room - 1)]

        put(mate(1), forward, (turn * rests + 1) * pair_most)

        @pl.loop(2, rests)
        def _(rest):
            put(mate(rest), forward, (turn * rests + rest) * pair_most)
            near_copy(turn, rest - 1, sender).start()

        put(me, landed, sender * pair_most)
        near_copy(turn, rests - 1, sender).start()

    def take(turn):
        out_copy(shifted(me, turn)).start()

        @pl.loop(1, rests)
        def _(rest):
            sender = shifted(mate(rest), turn)
            near_copy(turn, rest, sender).wait_recv()
            out_copy(sender).start()

    hand_on(0)
    for turn in (1, 2, 3):
        far_copy(turn).wait_recv()
        hand_on(turn)
        take(turn - 1)
    take(3)

    start = starts[me]
    length = spans[me]
    first_from = stretch[start] // blocks_dev
    last = jnp.maximum(length - 1, 0)
    last_from = stretch[start + last] // blocks_dev
    edge_out[0] = landed[last_from * pair_most + last // devices] * (
        wet[last] == 1
    ).astype(jnp.float32)
    edge_out[1] = landed[first_from * pair_most] * (wet[0] == 1).astype(jnp.float32)
    copies = []
    for side, shift in ((0, 1), (1, devices - 1)):
        copies.append(
            pltpu.make_async_remote_copy(
                src_ref=edge_out.at[side],
                dst_ref=edge_in.at[side],
                send_sem=edge_send.at[side],
                recv_sem=edge_recv.at[side],
                device_id=at((me + shift) % devices),
                device_id_type=MESH,
            )
        )
    for copy in copies:
        copy.start()
    for turn in range(4):
        if turn > 0:
            far_copy(turn).wait_send()

        @pl.loop(1, rests)
        def _(rest):
            near_copy(turn, rest, me).wait_send()

    @pl.loop(0, devices)
    def _(other):
        out_copy(other).wait()

    for copy in copies:
        copy.wait()
    final = pltpu.make_async_copy(edge_in, halo, edge_copy)
    final.start()
    final.wait()


def filter_kernel(sizes, chunk, stretch, spans, wet, counts, received, halo, out, rows, recips):
    groups, chips, pair_most, blocks_dev, all_blocks = sizes
    devices = groups * chips
    me = lax.axis_index("grp") * chips + lax.axis_index("dev")
    step = pl.program_id(0)
    length = spans[me]
    capacity = wet.shape[0]
    _, fields, cells = halo.shape

    @pl.when(step == 0)
    def _():
        start = lax.fori_loop(
            0, devices, lambda o, s: s + jnp.where(o < me, spans[o], 0), jnp.int32(0), unroll=8
        )

        def fill(spot, carry):
            rows[spot] = (stretch[jnp.minimum(start + spot, all_blocks - 1)] // blocks_dev) * pair_most
            return carry

        lax.fori_loop(0, devices, fill, jnp.int32(0), unroll=8)
        field = lax.broadcasted_iota(jnp.int32, (fields, cells), 0)
        held = jnp.ones((fields, cells), jnp.int32)
        for index in range(fields):
            held = jnp.where(field == index, counts[index], held)
        recips[...] = 0.25 / held.astype(jnp.float32)

    base = step * chunk
    scale = recips[...]
    lane = lax.broadcasted_iota(jnp.int32, (fields, cells), 1)
    at_first, at_last = lane == 0, lane == cells - 1
    left = halo[0] * jnp.where(me > 0, 1.0, 0.0)
    right = halo[1] * jnp.where(me < devices - 1, 1.0, 0.0)

    def wet_of(slot):
        return jnp.where(slot < length, wet[slot], 0).astype(jnp.float32)

    def block_of(slot, mask):
        return received[rows[lax.rem(slot, devices)] + lax.div(slot, devices)] * mask

    ahead = jnp.maximum(base - 1, 0)
    before = jnp.where(base == 0, left, block_of(ahead, wet_of(ahead)))
    mask = wet_of(base)
    here = block_of(base, mask)

    def one(offset, carry):
        before, here, mask = carry
        slot = base + offset
        later = jnp.minimum(slot + 1, capacity - 1)
        later_mask = wet_of(later)
        after = jnp.where(slot + 1 == length, right, block_of(later, later_mask))
        low = pltpu.roll(jnp.where(at_last, before, here), 1, 1)
        high = pltpu.roll(jnp.where(at_first, after, here), cells - 1, 1)
        out[offset] = (low + high + 2.0 * here) * (scale * mask)
        return here, after, later_mask

    lax.fori_loop(0, chunk, one, (before, here, mask), unroll=8)


def choose_kernel(sizes, rooms, spans, out):
    groups, chips, layers = sizes
    devices = groups * chips
    plane = chips // layers
    most = jnp.int32(0)
    for layer in range(layers):
        need = jnp.int32(0)
        for grp in range(groups):
            low = grp * chips + layer * plane
            part = lax.fori_loop(0, plane, lambda i, s, low=low: s + spans[low + i], jnp.int32(0))
            need = need + lax.div(part + devices - 1, devices)
        most = jnp.maximum(most, need)
    choice = jnp.int32(0)
    for room in rooms:
        choice = choice + jnp.where(most > room, 1, 0)
    out[0] = choice


def on_device(accum, step_count, stretch_slot, span_length, wet_mask):
    groups, chips = lax.axis_size("grp"), lax.axis_size("dev")
    devices = groups * chips
    blocks_dev, fields, cells = accum.shape
    capacity = wet_mask.shape[0]
    pair_most = capacity // devices
    all_blocks = stretch_slot.shape[0]
    layers = 4 if chips % 4 == 0 else 1
    smem = pl.BlockSpec(memory_space=pltpu.SMEM)
    vmem = pl.BlockSpec(memory_space=pltpu.VMEM)
    hbm = pl.BlockSpec(memory_space=pl.ANY)
    block = (fields, cells)
    f32 = jnp.float32
    sems = pltpu.SemaphoreType.DMA
    rows = pltpu.VMEM((capacity, *block), f32)
    pair = pltpu.VMEM((2, *block), f32)
    operands = (stretch_slot, span_length, wet_mask, accum)
    sizes = (groups, chips, layers, pair_most, blocks_dev, all_blocks)

    def exchange(kernel, scratch, number):
        return pl.pallas_call(
            kernel,
            out_shape=(
                jax.ShapeDtypeStruct((capacity, *block), f32),
                jax.ShapeDtypeStruct((2, *block), f32),
            ),
            in_specs=[smem, smem, smem, vmem],
            out_specs=(hbm, hbm),
            scratch_shapes=scratch,
            compiler_params=pltpu.CompilerParams(collective_id=number, has_side_effects=True),
        )

    def direct(*given):
        scratch = [pltpu.SMEM((devices,), jnp.int32), rows, rows, pair, pair]
        scratch += [sems((devices,))] * 3 + [sems((2,)), sems((2,)), sems]
        return exchange(functools.partial(exchange_kernel, sizes), scratch, 0)(*given)

    def relay(number, room):
        def run(*given):
            one = pltpu.VMEM((room, *block), f32)
            rests = devices // layers
            scratch = [pltpu.SMEM((devices + 1,), jnp.int32), pltpu.VMEM((3, room, *block), f32)]
            scratch += [one, one, one, pltpu.VMEM((4 * rests * pair_most, *block), f32), rows, pair, pair]
            scratch += [sems((3,)), sems((3,)), sems((4 * rests,)), sems((devices,)), sems((devices,))]
            scratch += [sems((2,)), sems((2,)), sems]
            return exchange(functools.partial(relay_kernel, sizes, room), scratch, number)(*given)

        return run

    if layers == 4 and groups == 2 and pair_most >= 8:
        most = (devices // layers) * pair_most
        rooms = [most * part // 64 for part in ROOMS]
        choice = pl.pallas_call(
            functools.partial(choose_kernel, (groups, chips, layers), rooms),
            out_shape=jax.ShapeDtypeStruct((1,), jnp.int32),
            in_specs=[smem],
            out_specs=smem,
        )(span_length)[0]
        branches = [relay(number + 1, room) for number, room in enumerate(rooms)] + [direct]
        received, halo = lax.switch(choice, branches, *operands)
    else:
        received, halo = direct(*operands)
    chunk = 32 if capacity % 32 == 0 else capacity
    return pl.pallas_call(
        functools.partial(
            filter_kernel, (groups, chips, pair_most, blocks_dev, all_blocks), chunk
        ),
        grid=(capacity // chunk,),
        out_shape=jax.ShapeDtypeStruct((capacity, *block), f32),
        in_specs=[smem, smem, smem, smem, vmem, vmem],
        out_specs=pl.BlockSpec((chunk, *block), lambda step: (step, 0, 0)),
        scratch_shapes=[pltpu.SMEM((devices,), jnp.int32), pltpu.VMEM(block, f32)],
    )(stretch_slot, span_length, wet_mask, step_count, received, halo)


def solution(mesh):
    return jax.shard_map(
        on_device,
        mesh=mesh,
        in_specs=(P(("grp", "dev"), None, None), P(), P(), P(), P(("grp", "dev"))),
        out_specs=P(("grp", "dev"), None, None),
        check_vma=False,
    )
```

profile of v0, /device:TPU:13, one launch (start us, length us, event | category | flops | bytes accessed | tf_op | source)
XLA Modules:
  0.0 72.1 jit_solution(12083758256896893148)
XLA Ops:
  0.0 1.4 %shard_map.55 = s32[1]{0:T(128)} custom-call(s32[32]{0:T(128)} %spans.3), custom_call_target="tpu_custom_call" | custom-call | tf_op jit(solution)/shard_map/pallas_call | solution.py:472
  2.1 62.9 %conditional.1 = ((f32[256,24,128]{2,1,0:T(8,128)S(1)}, f32[2,24,128]{2,1,0:T(8,128)S(1)})) conditional(s32[]{:T(128)} %bitcast, (s32[4096]{0:T(1024)}, s32[32]{0:T(128)}, s32[256]{0:T(256)}, f32[128,24,128]{2,1,0:T(8,128)}) %tuple.26, (s32[4096]{0:T(1024)}, s32[32]{0:T(128)}, s32[256]{0:T(256)}, ...), branch_computations={%region_0.0_spmd, %region_1.0_spmd, %region_2.0_spmd, %region_3.0_... | conditional | bytes 8 | solution.py:479
  2.1 62.9 %branch_2_fun.1 = (f32[256,24,128]{2,1,0:T(8,128)S(1)}, f32[2,24,128]{2,1,0:T(8,128)S(1)}) custom-call(s32[4096]{0:T(1024)} %get-tuple-element.69.stretch, s32[32]{0:T(128)} %get-tuple-element.70.spans, s32[256]{0:T(256)} %get-tuple-element.71.wet, f32[128,24,128]{2,1,0:T(8,128)} %get-tuple-element.72.accum), custom_call_target="tpu_custom_call" | custom-call | tf_op jit(solution)/shard_map/cond/branch_2_fun/pallas_call | solution.py:465
  65.0 7.1 %shard_map.56 = f32[256,24,128]{2,1,0:T(8,128)} custom-call(s32[4096]{0:T(1024)} %stretch.1, s32[32]{0:T(128)} %spans.3, s32[256]{0:T(256)} %wet.1, s32[24]{0:T(128)} %counts.1, f32[256,24,128]{2,1,0:T(8,128)S(1)} %get-tuple-element.91.received, f32[2,24,128]{2,1,0:T(8,128)S(1)} %get-tuple-element.92.halo), custom_call_target="tpu_custom_call" | custom-call | tf_op jit(solution)/shard_map/pallas_call | solution.py:483
where the time goes:
time: 73.1 us; the launch traced here: 72.1 us
  Pallas kernels  71.4 us (98%)
    pallas_call x1, Pallas kernels, run(): exchange(functools.partial(relay_kernel, sizes, room), scratch, number)  62.9 us
    pallas_call x1, Pallas kernels, on_device(): pl.pallas_call(functools.partial(filter_kernel, (groups, chips, pair_most...  7.08 us

commit v1 on v0

v1 whole, which is shorter than its diff:
```python
import functools
import jax
import jax.numpy as jnp
from jax import lax
from jax.experimental import pallas as pl
from jax.experimental.pallas import tpu as pltpu
from jax.sharding import PartitionSpec as P

MESH = pl.DeviceIdType.MESH
SPARES = ((4, 24), (6, 24), (8, 24), (10, 24), (12, 24), (14, 24), (16, 24), (20, 24), (12, 32), (20, 32), (32, 32))


def exchange_kernel(
    sizes, stretch, spans, wet, accum, received, halo,
    starts, packed, landed, edge_out, edge_in, send_sem, recv_sem, out_sem, edge_send, edge_recv, edge_copy,
):
    groups, chips, layers, pair_most, blocks_dev, all_blocks = sizes
    devices = groups * chips
    plane = chips // layers
    grp = lax.axis_index("grp")
    dev = lax.axis_index("dev")
    me = grp * chips + dev
    layer, place = dev // plane, dev % plane

    def at(index):
        return (index // chips, index % chips)

    barrier = pltpu.get_barrier_semaphore()

    @pl.loop(1, devices)
    def _(step):
        pl.semaphore_signal(barrier, inc=1, device_id=at((me + step) % devices), device_id_type=MESH)

    def prefix(owner, total):
        starts[owner] = total
        return total + spans[owner]

    lax.fori_loop(0, devices, prefix, jnp.int32(0))

    def find(block, found):
        return jnp.where(stretch[block] // blocks_dev == me, block, found)

    phase = lax.fori_loop(0, devices, find, jnp.int32(0), unroll=8)

    def partner(turn, rest):
        there = ((layer + turn) % layers) * plane + (place + rest % plane) % plane
        return ((grp + rest // plane) % groups) * chips + there

    def pack(owner, target, base):
        start = starts[owner]
        first = start + lax.rem(phase - start + all_blocks * devices, devices)
        for rank in range(pair_most):
            block = jnp.minimum(first + rank * devices, all_blocks - 1)
            slot = lax.rem(stretch[block], blocks_dev)
            target[base + rank] = accum[slot]

    def send_copy(other):
        return pltpu.make_async_remote_copy(
            src_ref=packed.at[pl.ds(other * pair_most, pair_most)],
            dst_ref=landed.at[pl.ds(me * pair_most, pair_most)],
            send_sem=send_sem.at[other],
            recv_sem=recv_sem.at[me],
            device_id=at(other),
            device_id_type=MESH,
        )

    def out_copy(other):
        return pltpu.make_async_copy(
            landed.at[pl.ds(other * pair_most, pair_most)],
            received.at[pl.ds(other * pair_most, pair_most)],
            out_sem.at[other],
        )

    turns = [layers // 2] + [t for t in range(1, layers) if t != layers // 2]
    if layers > 1:
        turns = turns + [0]
    else:
        turns = [0]
    rests = groups * plane
    for number, turn in enumerate(turns):
        low = 1 if turn == 0 else 0

        @pl.loop(low, rests)
        def _(rest):
            other = partner(turn, rest)
            pack(other, packed, other * pair_most)

        if number == 0:
            pl.semaphore_wait(barrier, devices - 1)

        @pl.loop(low, rests)
        def _(rest):
            send_copy(partner(turn, rest)).start()

    pack(me, landed, me * pair_most)

    for turn in reversed(turns):
        low = 1 if turn == 0 else 0

        @pl.loop(low, rests)
        def _(rest):
            other = partner(turn, rest)
            pltpu.make_async_remote_copy(
                src_ref=packed.at[pl.ds(other * pair_most, pair_most)],
                dst_ref=landed.at[pl.ds(other * pair_most, pair_most)],
                send_sem=send_sem.at[other],
                recv_sem=recv_sem.at[other],
                device_id=at(other),
                device_id_type=MESH,
            ).wait_recv()
            out_copy(other).start()

    out_copy(me).start()

    start = starts[me]
    length = spans[me]
    first_from = stretch[start] // blocks_dev
    last = jnp.maximum(length - 1, 0)
    last_from = stretch[start + last] // blocks_dev
    edge_out[0] = landed[last_from * pair_most + last // devices] * (
        wet[last] == 1
    ).astype(jnp.float32)
    edge_out[1] = landed[first_from * pair_most] * (wet[0] == 1).astype(jnp.float32)
    copies = []
    for side, shift in ((0, 1), (1, devices - 1)):
        copies.append(
            pltpu.make_async_remote_copy(
                src_ref=edge_out.at[side],
                dst_ref=edge_in.at[side],
                send_sem=edge_send.at[side],
                recv_sem=edge_recv.at[side],
                device_id=at((me + shift) % devices),
                device_id_type=MESH,
            )
        )
    for copy in copies:
        copy.start()

    @pl.loop(1, devices)
    def _(step):
        send_copy((me + step) % devices).wait_send()

    @pl.loop(0, devices)
    def _(other):
        out_copy(other).wait()

    for copy in copies:
        copy.wait()
    final = pltpu.make_async_copy(edge_in, halo, edge_copy)
    final.start()
    final.wait()


def stream_kernel(
    sizes, spare, early, stretch, spans, wet, accum_at, received, halo,
    starts, accum, to_mate, to_spare, to_near, to_far, lists, merged, forward, edge_all, edge_near,
    load_sem, mate_send, mate_recv, spare_send, spare_recv, pass_send, main_send, main_recv,
    near_send, near_recv, edge_send, edge_recv,
):
    groups, chips, layers, pair_most, blocks_dev, all_blocks = sizes
    devices = groups * chips
    plane = chips // layers
    rests = groups * plane
    main = rests * pair_most // 2
    room = main + spare
    _, fields, cells = accum.shape
    shift = devices.bit_length() - 1
    grp = lax.axis_index("grp")
    dev = lax.axis_index("dev")
    me = grp * chips + dev
    layer, place = dev // plane, dev % plane
    low = layer < 2
    inner = (layer == 1) | (layer == 2)
    across = (
        layer, layer + 1 - 2 * (layer % 2), jnp.where(low, 2, 1), jnp.where(low, 3, 0)
    )
    my_spot = grp * plane + place

    def at(index):
        return (index // chips, index % chips)

    def column(there):
        return grp * chips + there * plane + place

    def mate(spot):
        return (spot // plane) * chips + layer * plane + spot % plane

    load = pltpu.make_async_copy(accum_at, accum, load_sem)
    load.start()
    barrier = pltpu.get_barrier_semaphore()
    for turn in (1, 2, 3):
        pl.semaphore_signal(
            barrier, inc=1, device_id=at(column((layer + turn) % layers)), device_id_type=MESH
        )

    @pl.loop(1, rests)
    def _(step):
        pl.semaphore_signal(
            barrier, inc=1, device_id=at(mate((my_spot + step) % rests)), device_id_type=MESH
        )

    def prefix(owner, total):
        starts[owner] = total
        return total + spans[owner]

    starts[devices] = lax.fori_loop(0, devices, prefix, jnp.int32(0), unroll=8)

    def find(block, found):
        holder = lax.div(stretch[block], blocks_dev)
        return tuple(
            jnp.where(holder == column(across[turn]), block, found[turn]) for turn in range(4)
        )

    phases = lax.fori_loop(0, devices, find, (jnp.int32(0),) * 4, unroll=8)

    def rank_of(phase, owner):
        return lax.shift_right_arithmetic(starts[owner] + (devices - 1) - phase, jnp.int32(shift))

    def layer_list(phase, there):
        marks = []
        for part in range(2):
            first = part * chips + there * plane
            begin = rank_of(phase, first)
            marks.append((begin, rank_of(phase, first + plane) - begin))
        (begin_low, amount), (begin_high, more) = marks
        return amount, begin_low, begin_high - amount, amount + more

    def slot_of(rank, phase):
        block = jnp.minimum(phase + rank * devices, all_blocks - 1)
        return lax.rem(stretch[block], blocks_dev)

    mine = phases[0]
    lists_to = [layer_list(mine, across[turn]) for turn in range(4)]

    def block_at(listed, spot):
        amount, begin_low, begin_high, _ = listed
        return accum[slot_of(spot + jnp.where(spot < amount, begin_low, begin_high), mine)]

    def fill(target, begin, end, listed):
        def one(spot, carry):
            target[spot] = block_at(listed, spot)
            return carry

        lax.fori_loop(begin, end, one, jnp.int32(0), unroll=4)

    far_list = jnp.where(inner, 1, 2)

    def pick(turn, values):
        if turn == "first":
            return jnp.where(inner, values[2], values[3])
        if turn == "second":
            return jnp.where(inner, values[3], values[2])
        return values[turn]

    def order(turn):
        return {"first": 2, "second": 3}.get(turn, turn)

    def mate_copy(step):
        begin, end = ((0, early), (early, room + 1))[step]
        return pltpu.make_async_remote_copy(
            src_ref=to_mate.at[pl.ds(begin, end - begin)],
            dst_ref=lists.at[0, pl.ds(begin, end - begin)],
            send_sem=mate_send.at[step],
            recv_sem=mate_recv.at[step],
            device_id=at(column(across[1])),
            device_id_type=MESH,
        )

    def spare_copy(where):
        return pltpu.make_async_remote_copy(
            src_ref=to_spare,
            dst_ref=lists.at[where, pl.ds(main, spare + 1)],
            send_sem=spare_send,
            recv_sem=spare_recv.at[where],
            device_id=at(column(across[2])),
            device_id_type=MESH,
        )

    def pass_copy(where):
        return pltpu.make_async_remote_copy(
            src_ref=lists.at[where, pl.ds(main, spare + 1)],
            dst_ref=lists.at[where, pl.ds(main, spare + 1)],
            send_sem=pass_send.at[where],
            recv_sem=spare_recv.at[where],
            device_id=at(column(across[1])),
            device_id_type=MESH,
        )

    cuts = [(0, early), (early, main)] if early < main else [(0, main)]

    def main_copy(outer, step, where):
        begin, end = cuts[step]
        return pltpu.make_async_remote_copy(
            src_ref=(to_far if outer else to_near).at[pl.ds(begin, end - begin)],
            dst_ref=lists.at[where, pl.ds(begin, end - begin)],
            send_sem=main_send.at[outer, step],
            recv_sem=main_recv.at[where, step],
            device_id=at(column(across[3 if outer else 2])),
            device_id_type=MESH,
        )

    def near_copy(turn, spot, sender):
        return pltpu.make_async_remote_copy(
            src_ref=forward.at[pl.ds((order(turn) * rests + spot) * pair_most, pair_most)],
            dst_ref=received.at[pl.ds(sender * pair_most, pair_most)],
            send_sem=near_send.at[order(turn) * rests + spot],
            recv_sem=near_recv.at[sender],
            device_id=at(mate(spot)),
            device_id_type=MESH,
        )

    def edge_copy(spot, sender):
        return pltpu.make_async_remote_copy(
            src_ref=edge_all,
            dst_ref=edge_near.at[sender],
            send_sem=edge_send.at[spot],
            recv_sem=edge_recv.at[sender],
            device_id=at(mate(spot)),
            device_id_type=MESH,
        )

    def hand_on(turn, begin, end, limit):
        listed = pick(turn, (0, 0, 1, 2))
        phase = pick(turn, phases)
        sender = column(pick(turn, across))
        if turn != 0:
            amount, begin_low, begin_high, _ = layer_list(phase, layer)
            jump = jnp.int32(0)
            if turn != 1:
                other = layer_list(phase, across[1])[3]
                jump = jnp.where(inner, jnp.maximum(other - main, 0), 0)

        def put(spot, target, base):
            owner = mate(spot)
            first = rank_of(phase, owner)
            if turn != 0:
                first = first - jnp.where(spot < plane, begin_low, begin_high)
            for step in range(pair_most):
                if turn == 0:
                    target[base + step] = accum[slot_of(first + step, phase)]
                else:
                    row = first + step
                    if turn != 1:
                        row = row + jnp.where(row < main, 0, jump)
                    target[base + step] = merged[listed, jnp.clip(row, 0, limit - 1)]

        @pl.loop(begin, end)
        def _(spot):
            @pl.when(spot != my_spot)
            def _():
                put(spot, forward, (order(turn) * rests + spot) * pair_most)

            @pl.when(spot == my_spot)
            def _():
                put(spot, received, sender * pair_most)

        @pl.loop(begin, end)
        def _(spot):
            @pl.when(spot != my_spot)
            def _():
                near_copy(turn, spot, sender).start()

    load.wait()
    fill(to_mate, 0, early, lists_to[1])

    @pl.when(inner)
    def _():
        fill(to_near, 0, cuts[0][1], lists_to[2])

    pl.semaphore_wait(barrier, layers - 1 + rests - 1)
    mate_copy(0).start()

    @pl.when(inner)
    def _():
        main_copy(0, 0, far_list).start()

    hand_on(0, 0, rests, None)

    lane = lax.broadcasted_iota(jnp.int32, (fields, cells), 1)
    ending = jnp.maximum(spans[me] - 1, 0)
    edges = jnp.where(
        lane == 2 * (devices + me),
        jnp.where(wet[0] == 1, 1.0, 0.0),
        jnp.where(
            lane == 2 * (devices + me) + 1, jnp.where(wet[ending] == 1, 1.0, 0.0), 0.0
        ),
    )

    def collect(owner, edges):
        for back, turned in ((1, 2 * owner), (0, 2 * owner - 1)):
            held = stretch[jnp.clip(starts[owner] - back, 0, all_blocks - 1)]
            rolled = pltpu.roll(accum[lax.rem(held, blocks_dev)], (turned + back) % cells, 1)
            wanted = jnp.where(lax.div(held, blocks_dev) == me, turned, -1)
            edges = jnp.where(lane == wanted, rolled, edges)
        return edges

    edges = lax.fori_loop(1, devices, collect, edges, unroll=2)
    to_mate[room] = edges
    to_spare[spare] = edges
    over = jnp.maximum(lists_to[3][3] - main, 0)

    def fill_spare(spot, carry):
        rank = []
        for listed, back in ((lists_to[3], 0), (lists_to[2], over)):
            amount, begin_low, begin_high, _ = listed
            there = main + spot - back
            rank.append(there + jnp.where(there < amount, begin_low, begin_high))
        to_spare[spot] = accum[slot_of(jnp.where(spot < over, rank[0], rank[1]), mine)]
        return carry

    lax.fori_loop(0, spare, fill_spare, jnp.int32(0), unroll=2)
    fill(to_mate, early, room, lists_to[1])
    spare_copy(far_list).start()
    mate_copy(1).start()
    last = len(cuts) - 1

    @pl.when(inner)
    def _():
        fill(to_far, 0, main, lists_to[3])
        for step in range(last + 1):
            main_copy(1, step, far_list).start()
        if last:
            fill(to_near, cuts[1][0], main, lists_to[2])
            main_copy(0, 1, far_list).start()

    @pl.when(jnp.logical_not(inner))
    def _():
        for step in range(last + 1):
            fill(to_far, *cuts[step], lists_to[3])
            fill(to_near, *cuts[step], lists_to[2])
            main_copy(1, step, far_list).start()
            main_copy(0, step, far_list).start()

    near_group = (0, plane, early) if last else (0, rests, room)
    far_group = (plane, rests, room)

    def merge(where, begin, end):
        part = pl.ds(begin, end - begin)
        merged[where, part] = lists[where, part]

    def arrive(where, step):
        main_copy(0, step, where).wait_recv()
        merge(where, *cuts[step])

    def spared(where):
        spare_copy(where).wait_recv()
        merge(where, main, room)

    @pl.when(inner)
    def _():
        spared(1)
        pass_copy(1).start()
        spared(2)
        pass_copy(2).start()

    mate_copy(0).wait_recv()
    merge(0, 0, early)
    hand_on(1, 0, plane, early)

    @pl.when(inner)
    def _():
        arrive(1, 0)
        hand_on(2, *near_group)

    mate_copy(1).wait_recv()
    merge(0, early, room)
    hand_on(1, plane, rests, room)

    @pl.when(jnp.logical_not(inner))
    def _():
        spared(2)

    arrive(2, 0)
    hand_on(3, *near_group)
    if last:
        arrive(2, 1)
        hand_on(3, *far_group)

    @pl.when(jnp.logical_not(inner))
    def _():
        spared(1)

    total = edges
    for where in range(3):
        total = total + lists[where, room]
    edge_all[...] = total

    @pl.loop(0, rests)
    def _(spot):
        @pl.when(spot != my_spot)
        def _():
            edge_copy(spot, my_spot).start()

    @pl.when(jnp.logical_not(inner))
    def _():
        arrive(1, 0)
        hand_on(2, *near_group)

    if last:
        arrive(1, 1)
        hand_on(2, *far_group)

    @pl.when(inner)
    def _():
        for where in (1, 2):
            pass_copy(where).wait_send()

    for step in range(2):
        mate_copy(step).wait_send()
    spare_copy(far_list).wait_send()
    for outer in range(2):
        for step in range(last + 1):
            main_copy(outer, step, far_list).wait_send()

    edge_near[my_spot] = total

    @pl.loop(0, rests)
    def _(spot):
        @pl.when(spot != my_spot)
        def _():
            edge_copy(spot, spot).wait()

    total = edge_near[0]
    for spot in range(1, rests):
        total = total + edge_near[spot]
    spread = cells * devices

    def cell(to, lane_from):
        return pltpu.roll(total, lax.rem(to - lane_from + spread, cells), 1)

    wet_left, wet_right = 2 * (devices + me) - 1, 2 * (devices + me) + 2
    halo[0] = cell(cells - 1, 2 * me) * cell(cells - 1, wet_left)
    halo[1] = cell(0, 2 * me + 1) * cell(0, wet_right)

    @pl.loop(0, rests)
    def _(spot):
        @pl.when(spot != my_spot)
        def _():
            for turn in range(4):
                sender = (spot // plane) * chips + across[turn] * plane + spot % plane
                near_copy(turn, spot, sender).wait()


def filter_kernel(sizes, stretch, spans, wet, counts, received, halo, out, rows, done, sem):
    groups, chips, pair_most, blocks_dev, all_blocks = sizes
    devices = groups * chips
    me = lax.axis_index("grp") * chips + lax.axis_index("dev")
    length = spans[me]
    capacity = wet.shape[0]
    _, fields, cells = halo.shape
    start = lax.fori_loop(
        0, devices, lambda o, s: s + jnp.where(o < me, spans[o], 0), jnp.int32(0), unroll=8
    )

    def fill(spot, carry):
        block = jnp.minimum(start + spot, all_blocks - 1)
        rows[spot] = lax.div(stretch[block], blocks_dev) * pair_most
        return carry

    lax.fori_loop(0, devices, fill, jnp.int32(0), unroll=8)
    rows[devices] = rows[0] + 1
    field = lax.broadcasted_iota(jnp.int32, (fields, cells), 0)
    held = jnp.ones((fields, cells), jnp.int32)
    for index in range(fields):
        held = jnp.where(field == index, counts[index], held)
    scale = 0.25 / held.astype(jnp.float32)
    lane = lax.broadcasted_iota(jnp.int32, (fields, cells), 1)
    at_first, at_last = lane == 0, lane == cells - 1
    left = halo[0] * jnp.where(me > 0, 1.0, 0.0)
    right = halo[1] * jnp.where(me < devices - 1, 1.0, 0.0)

    def wet_of(slot):
        return jnp.where(slot < length, wet[slot], 0).astype(jnp.float32)

    def out_copy(rank):
        part = pl.ds(rank * devices, devices)
        return pltpu.make_async_copy(done.at[part], out.at[part], sem.at[rank])

    def one_rank(rank, carry):
        def one(spot, carry):
            before, here, mask = carry
            slot = rank * devices + spot
            later = jnp.minimum(slot + 1, capacity - 1)
            later_mask = wet_of(later)
            row = jnp.minimum(rows[spot + 1] + rank, capacity - 1)
            after = jnp.where(slot + 1 == length, right, received[row] * later_mask)
            low = pltpu.roll(jnp.where(at_last, before, here), 1, 1)
            high = pltpu.roll(jnp.where(at_first, after, here), cells - 1, 1)
            done[slot] = (low + high + 2.0 * here) * (scale * mask)
            return here, after, later_mask

        carry = lax.fori_loop(0, devices, one, carry, unroll=8)
        out_copy(rank).start()
        return carry

    mask = wet_of(jnp.int32(0))
    lax.fori_loop(0, pair_most, one_rank, (left, received[rows[0]] * mask, mask))

    @pl.loop(0, pair_most)
    def _(rank):
        out_copy(rank).wait()


def choose_kernel(sizes, main, spares, spans, out):
    groups, chips, layers = sizes
    devices = groups * chips
    plane = chips // layers
    over, most = [], jnp.int32(0)
    for layer in range(layers):
        need = jnp.int32(0)
        for grp in range(groups):
            part = jnp.int32(0)
            for spot in range(plane):
                part = part + spans[grp * chips + layer * plane + spot]
            part = lax.div(part + devices - 1, devices)
            if grp == 0:
                most = jnp.maximum(most, part)
            need = need + part
        over.append(jnp.maximum(need - main, 0))
    need = jnp.maximum(over[0] + over[1], over[2] + over[3])
    choice = jnp.int32(len(spares))
    for number, (spare, early) in reversed(list(enumerate(spares))):
        choice = jnp.where((need <= spare) & (most <= early), number, choice)
    out[0] = choice


def on_device(accum, step_count, stretch_slot, span_length, wet_mask):
    groups, chips = lax.axis_size("grp"), lax.axis_size("dev")
    devices = groups * chips
    blocks_dev, fields, cells = accum.shape
    capacity = wet_mask.shape[0]
    pair_most = capacity // devices
    all_blocks = stretch_slot.shape[0]
    layers = 4 if chips % 4 == 0 else 1
    smem = pl.BlockSpec(memory_space=pltpu.SMEM)
    vmem = pl.BlockSpec(memory_space=pltpu.VMEM)
    hbm = pl.BlockSpec(memory_space=pl.ANY)
    block = (fields, cells)
    f32 = jnp.float32
    sems = pltpu.SemaphoreType.DMA
    rows = pltpu.VMEM((capacity, *block), f32)
    pair = pltpu.VMEM((2, *block), f32)
    shapes = (
        jax.ShapeDtypeStruct((capacity, *block), f32),
        jax.ShapeDtypeStruct((2, *block), f32),
    )
    operands = (stretch_slot, span_length, wet_mask, accum)
    sizes = (groups, chips, layers, pair_most, blocks_dev, all_blocks)

    def exchange(kernel, scratch, number):
        return pl.pallas_call(
            kernel,
            out_shape=shapes,
            in_specs=[smem, smem, smem, vmem],
            out_specs=(hbm, hbm),
            scratch_shapes=scratch,
            compiler_params=pltpu.CompilerParams(collective_id=number, has_side_effects=True),
        )

    def direct(*given):
        scratch = [pltpu.SMEM((devices,), jnp.int32), rows, rows, pair, pair]
        scratch += [sems((devices,))] * 3 + [sems((2,)), sems((2,)), sems]
        return exchange(functools.partial(exchange_kernel, sizes), scratch, 0)(*given)

    def stream(number, spare, early):
        def run(*given):
            rests = devices // layers
            main = rests * pair_most // 2
            room = main + spare

            def many(*count):
                return pltpu.VMEM((*count, *block), f32)

            scratch = [pltpu.SMEM((devices + 1,), jnp.int32), many(blocks_dev), many(room + 1)]
            scratch += [many(spare + 1), many(main), many(main), many(3, room + 1), many(3, room)]
            scratch += [many(4 * rests * pair_most), many(), many(rests)]
            scratch += [sems, sems((2,)), sems((2,)), sems, sems((3,)), sems((3,))]
            scratch += [sems((2, 2)), sems((3, 2)), sems((4 * rests,)), sems((devices,))]
            scratch += [sems((rests,)), sems((rests,))]
            return pl.pallas_call(
                functools.partial(stream_kernel, sizes, spare, early),
                out_shape=shapes,
                in_specs=[smem, smem, smem, hbm],
                out_specs=(vmem, vmem),
                scratch_shapes=scratch,
                compiler_params=pltpu.CompilerParams(collective_id=number, has_side_effects=True),
            )(*given)

        return run

    ready = devices & (devices - 1) == 0 and 4 * devices <= cells
    if layers == 4 and groups == 2 and pair_most >= 8 and ready:
        main = (devices // layers) * pair_most // 2
        spares = [(main * spare // 32, main * early // 32) for spare, early in SPARES]
        choice = pl.pallas_call(
            functools.partial(choose_kernel, (groups, chips, layers), main, spares),
            out_shape=jax.ShapeDtypeStruct((1,), jnp.int32),
            in_specs=[smem],
            out_specs=smem,
        )(span_length)[0]
        branches = [stream(number + 1, *spare) for number, spare in enumerate(spares)] + [direct]
        received, halo = lax.switch(choice, branches, *operands)
    else:
        received, halo = direct(*operands)
    return pl.pallas_call(
        functools.partial(filter_kernel, (groups, chips, pair_most, blocks_dev, all_blocks)),
        out_shape=shapes[0],
        in_specs=[smem, smem, smem, smem, vmem, vmem],
        out_specs=hbm,
        scratch_shapes=[pltpu.SMEM((devices + 1,), jnp.int32), rows, sems((pair_most,))],
    )(stretch_slot, span_length, wet_mask, step_count, received, halo)


def solution(mesh):
    return jax.shard_map(
        on_device,
        mesh=mesh,
        in_specs=(P(("grp", "dev"), None, None), P(), P(), P(), P(("grp", "dev"))),
        out_specs=P(("grp", "dev"), None, None),
        check_vma=False,
    )
```

time: 73.1 us -> 68.5 us (0.937)
  the two profiles are of different devices: /device:TPU:13 before, /device:TPU:1 now
where the time goes in v1:
time: 68.5 us; the launch traced here: 68.2 us
  Pallas kernels  67.1 us (98%)
  between operations  0.83 us (1%)
    pallas_call x1, Pallas kernels, run(): pl.pallas_call(functools.partial(stream_kernel, sizes, spare, early), out...  59.9 us
    pallas_call x1, Pallas kernels, on_device(): pl.pallas_call(functools.partial(filter_kernel, (groups, chips, pair_most...  6.01 us

profile of v1, /device:TPU:1, one launch (start us, length us, event | category | flops | bytes accessed | tf_op | source)
XLA Modules:
  0.0 68.2 jit_solution(11970133316480945733)
XLA Ops:
  0.0 1.2 %shard_map.55 = s32[1]{0:T(128)} custom-call(s32[32]{0:T(128)} %spans.3), custom_call_target="tpu_custom_call" | custom-call | tf_op jit(solution)/shard_map/pallas_call | solution.py:695
  1.9 60.1 %conditional.1 = ((f32[256,24,128]{2,1,0:T(8,128)S(1)}, f32[2,24,128]{2,1,0:T(8,128)S(1)})) conditional(s32[]{:T(128)} %bitcast, (s32[4096]{0:T(1024)}, s32[32]{0:T(128)}, s32[256]{0:T(256)}, f32[128,24,128]{2,1,0:T(8,128)}) %tuple.41, (s32[4096]{0:T(1024)}, s32[32]{0:T(128)}, s32[256]{0:T(256)}, ...), branch_computations={%region_0.0_spmd, %region_1.0_spmd, %region_2.0_spmd, %region_3.0_... | conditional | bytes 8 | solution.py:702
  1.9 59.9 %branch_4_fun.1 = (f32[256,24,128]{2,1,0:T(8,128)S(1)}, f32[2,24,128]{2,1,0:T(8,128)S(1)}) custom-call(s32[4096]{0:T(1024)} %get-tuple-element.117.stretch, s32[32]{0:T(128)} %get-tuple-element.118.spans, s32[256]{0:T(256)} %get-tuple-element.119.wet, f32[128,24,128]{2,1,0:T(8,128)} %get-tuple-element.120.accum_at), custom_call_target="tpu_custom_call" | custom-call | tf_op jit(solution)/shard_map/cond/branch_4_fun/pallas_call | solution.py:680
  62.0 6.0 %shard_map.56 = f32[256,24,128]{2,1,0:T(8,128)} custom-call(s32[4096]{0:T(1024)} %stretch.1, s32[32]{0:T(128)} %spans.3, s32[256]{0:T(256)} %wet.1, s32[24]{0:T(128)} %counts.1, f32[256,24,128]{2,1,0:T(8,128)S(1)} %get-tuple-element.151.received, f32[2,24,128]{2,1,0:T(8,128)S(1)} %get-tuple-element.152.halo), custom_call_target="tpu_custom_call" | custom-call | tf_op jit(solution)/shard_map/pallas_call | solution.py:705
